TPU v7x, 32 devices: a whole 2x2x4 slice. The times are simulated.
32 devices in a mesh: dp: 8 (over z, x), zero: 4 (over y, core).
Axes of the slice: x: 2, y: 2, z: 4, core: 2. Of those that a mesh axis runs over, the one named last changes fastest.
Arguments:
- tokens: float32 [32768, 768], P(('dp', 'zero')), may hold values from -6 to 6
- cotangent: float32 [32768, 768], P(('dp', 'zero')), may hold values from -6 to 6
- lengths: int32 [32], P(('dp', 'zero')), may hold values from 0 to 1024, as said below
- master_matrix: float32 [9216, 768], P(('dp', 'zero')), may hold values from -2 to 2
- master_vector: float32 [12, 768], P(None, ('dp', 'zero')), may hold values from -2 to 2
- moment_matrix: float32 [9216, 768], P(('dp', 'zero')), may hold values from -2 to 2
- moment_vector: float32 [12, 768], P(None, ('dp', 'zero')), may hold values from -2 to 2
- square_matrix: float32 [9216, 768], P(('dp', 'zero')), may hold values from 0.01 to 0.3
- square_vector: float32 [12, 768], P(None, ('dp', 'zero')), may hold values from 0.01 to 0.3
Outputs:
- block_out: float32 [32768, 768], P(('dp', 'zero'))
- input_gradient: float32 [32768, 768], P(('dp', 'zero'))
- matrix_gradient: float32 [9216, 768], P(('dp', 'zero'))
- vector_gradient: float32 [12, 768], P(None, ('dp', 'zero'))
- matrix_weights: float32 [9216, 768], P(('dp', 'zero'))
- vector_weights: float32 [12, 768], P(None, ('dp', 'zero'))
- matrix_moment: float32 [9216, 768], P(('dp', 'zero'))
- vector_moment: float32 [12, 768], P(None, ('dp', 'zero'))
- matrix_square: float32 [9216, 768], P(('dp', 'zero'))
- vector_square: float32 [12, 768], P(None, ('dp', 'zero'))
Inputs may be any that keep to these rules, and one draw needn't show every extreme that they name: A slot holds a sequence of lengths tokens from its start; 0 marks an empty slot; nonzero lengths are at least 512, and some slot has exactly 1024.
All inputs are finite; a program needn't handle non-finite values.
Results may differ from a plain program's by a relative error of at most 0.012.
Values may be sent and summed in bfloat16 or wider, within the bound.
A program may use at most 256 MiB of HBM per device.

v0:
```python
import functools
import jax, jax.numpy as jnp
from jax import lax
from jax.experimental import pallas as pl
from jax.experimental.pallas import tpu as pltpu
from jax.sharding import PartitionSpec as P

f32, bf16 = jnp.float32, jnp.bfloat16
D = 768
SEQ = 1024
PAIRS = 6
FF = 3072
EPS = 1e-05
NEG = -1e30
CUBIC = 0.044715
ROOT = 0.7978845608028654
QB = 256
NT = (((1,), (1,)), ((), ()))
NN = (((1,), (0,)), ((), ()))
TN = (((0,), (0,)), ((), ()))


def dot(a, b, dn):
    return lax.dot_general(a, b, dn, preferred_element_type=f32)


def cuts(rows, parts):
    marks = [8 * round(rows * h / parts / 8) for h in range(parts + 1)]
    return [(marks[h], marks[h + 1] - marks[h]) for h in range(parts)]


class Place:
    def __init__(self, n_dp):
        self.na = n_dp // 2
        dp, zero = lax.axis_index("dp"), lax.axis_index("zero")
        self.a, self.b, self.y, self.c = dp // 2, dp % 2, zero // 2, zero % 2

    def sid(self, a, b, y, c):
        return ((a * 2 + b) * 2 + y) * 2 + c

    def dev(self, a, b, y, c):
        return {"dp": a * 2 + b, "zero": y * 2 + c}

    def x_mate(self):
        return self.dev(self.a, 1 - self.b, self.y, self.c)

    def y_mate(self):
        return self.dev(self.a, self.b, 1 - self.y, self.c)

    def core_mate(self):
        return self.dev(self.a, self.b, self.y, 1 - self.c)

    def at(self, a):
        return self.dev(a, self.b, self.y, self.c)


def greet(me):
    barrier = pltpu.get_barrier_semaphore()
    for peer in (me.x_mate(), me.y_mate(), me.core_mate()):
        pl.semaphore_signal(barrier, inc=1, device_id=peer)
    for i in range(1, me.na):
        pl.semaphore_signal(barrier, inc=1, device_id=me.at((me.a + i) % me.na))
    pl.semaphore_wait(barrier, me.na + 2)


FINE = 4
HALVES = 2


def forward_kernel(
    n_dp, lengths, tokens_in, master_in, vector_in, cot_in,
    whole, ge, n1_out, qkv_out, mixed_out, low_out, base_out, block_out, vec, lse, part_sums,
    tokens, master, vector, cot, load_sem, save_sem,
    n1, qkv, mixed, low, after, acc, ngrad, n2, top_low, act, hid, w_out, wf, wd, w_sem, stage, stage_sem,
    own, own_sem, wq, wq_sem, tile, tiles_in, vin, vtmp, vs_sem, vr_sem, lc,
    ch_s, ch_r, up_s, dn_s, ds, xs, xr, ys, yr, fs, fr, ks, kr,
):
    me = Place(n_dp)
    na = me.na
    nq = na // 4
    a, b, y, c = me.a, me.b, me.y, me.c
    rows = master.shape[0]
    relay = na == 4
    around = ((b, y), (1 - b, y), (b, 1 - y), (1 - b, 1 - y))

    def remote(s, h, n, send, recv, peer):
        first, size = cuts(rows, n)[h]
        ref = whole.at[pl.ds(pl.multiple_of(s * rows + first, 8), size)]
        return pltpu.make_async_remote_copy(
            src_ref=ref, dst_ref=ref, send_sem=send, recv_sem=recv, device_id=peer
        )

    def chain_down(a_, h):
        return remote(me.sid(a_, b, y, c), h, FINE, ch_s.at[a_, h], ch_r.at[a_, h], me.at(a - 1))

    def chain_up(a_, h):
        return remote(me.sid(a_, b, y, c), h, FINE, ch_s.at[na + a_, h], ch_r.at[a_, h], me.at(a + 1))

    def direct(to):
        return remote(me.sid(a, b, y, c), 0, 1, ds.at[to], ch_r.at[a, 0], me.at(to))

    def direct_from(a_):
        return remote(me.sid(a_, b, y, c), 0, 1, ds.at[a_], ch_r.at[a_, 0], me.at(a_))

    def x_copy(a_, h, n, mine=True):
        return remote(me.sid(a_, b if mine else 1 - b, y, c), h, n, xs.at[a_, h], xr.at[a_, h], me.x_mate())

    def y_copy(a_, h, n, mine=True):
        return remote(me.sid(a_, b, y if mine else 1 - y, c), h, n, ys.at[a_, h], yr.at[a_, h], me.y_mate())

    def diag_send(a_, h, n):
        if h < n // 2:
            return remote(me.sid(a_, 1 - b, y, c), h, n, fs.at[a_, h], fr.at[a_, h], me.y_mate())
        return remote(me.sid(a_, b, 1 - y, c), h, n, fs.at[a_, h], fr.at[a_, h], me.x_mate())

    def diag_recv(a_, h, n):
        return remote(me.sid(a_, 1 - b, 1 - y, c), h, n, fs.at[a_, h], fr.at[a_, h], me.x_mate())

    def core(a_, b_, y_, h, n, mine=True):
        o = (b_ + b) % 2 + 2 * ((y_ + y) % 2)
        return remote(
            me.sid(a_, b_, y_, c if mine else 1 - c), h, n, ks.at[a_, o, h], kr.at[a_, o, h], me.core_mate()
        )

    def column_sends(a_, h, n):
        x_copy(a_, h, n).start()
        y_copy(a_, h, n).start()
        core(a_, b, y, h, n).start()

    def pass_chain(h):
        for a_ in range(nq):
            @pl.when(a != a_)
            def _():
                chain_up(a_, h).wait_recv()

                @pl.when((a_ < a) & (a + 1 < na))
                def _():
                    chain_up(a_, h).start()

                @pl.when((a_ > a) & (a > 0))
                def _():
                    chain_down(a_, h).start()

                column_sends(a_, h, FINE)

    def relay_up(a_):
        return remote(me.sid(a_, b, y, c), 0, 1, up_s.at[a_], ch_r.at[a_, 0], me.at(a + 1))

    def relay_down(a_):
        return remote(me.sid(a_, b, y, c), 0, 1, dn_s.at[a_], ch_r.at[a_, 0], me.at(a - 1))

    def take(a_):
        direct_from(a_).wait_recv()
        if relay:
            @pl.when((a_ < a) & (a + 1 < na))
            def _():
                relay_up(a_).start()

            @pl.when((a_ > a) & (a > 0))
            def _():
                relay_down(a_).start()

    def take_at(k):
        a_ = a + k

        @pl.when((a_ >= nq) & (a_ < na))
        def _():
            take(a_)

    def share(a_):
        for h in range(HALVES):
            column_sends(a_, h, HALVES)

    def pass_plane(a_, n):
        for h in range(n):
            x_copy(a_, h, n, False).wait_recv()
            if h < n // 2:
                diag_send(a_, h, n).start()
            core(a_, 1 - b, y, h, n).start()
            y_copy(a_, h, n, False).wait_recv()
            if h >= n // 2:
                diag_send(a_, h, n).start()
            core(a_, b, 1 - y, h, n).start()

    def pass_diag(a_, n):
        for h in range(n):
            diag_recv(a_, h, n).wait_recv()
            core(a_, 1 - b, 1 - y, h, n).start()

    def partner(a_, n):
        for b_, y_ in around:
            for h in range(n):
                core(a_, b_, y_, h, n, False).wait_recv()

    def load(k, src, dst):
        return pltpu.make_async_copy(src, dst, load_sem.at[k])

    loads = [load(0, master_in, master), load(1, vector_in, vector), load(2, tokens_in, tokens), load(3, cot_in, cot)]
    for one in loads:
        one.start()
    mine = me.sid(a, b, y, c)
    columns = vector.shape[1]
    loads[0].wait()
    loads[1].wait()
    own[...] = master[...].astype(bf16)
    put = pltpu.make_async_copy(own, whole.at[pl.ds(pl.multiple_of(mine * rows, 8), rows)], own_sem)
    put.start()
    narrow = (
        lax.broadcasted_iota(jnp.int32, (columns, 128), 1) == lax.broadcasted_iota(jnp.int32, (columns, 128), 0)
    ).astype(bf16)
    tile[0:12, :] = dot(vector[...].astype(bf16), narrow, NN)
    tile[12:16, :] = jnp.zeros((4, 128), f32)

    def widen(small, s):
        move = (
            lax.broadcasted_iota(jnp.int32, (128, D), 1) == lax.broadcasted_iota(jnp.int32, (128, D), 0) + s * columns
        ) & (lax.broadcasted_iota(jnp.int32, (128, D), 0) < columns)
        return dot(small.astype(bf16), move.astype(bf16), NN)

    greet(me)
    put.wait()

    def vec_copy(i, k, peer):
        return pltpu.make_async_remote_copy(
            src_ref=vin.at[i], dst_ref=vtmp.at[k], send_sem=vs_sem.at[k], recv_sem=vr_sem.at[k], device_id=peer
        )

    def vec_at(i):
        return pltpu.make_async_remote_copy(
            src_ref=tile, dst_ref=tiles_in.at[i], send_sem=vs_sem.at[2 + i], recv_sem=vr_sem.at[2 + i],
            device_id=me.at((a + i) % na),
        )

    v_y, v_x, v_core = vec_copy(1, 0, me.y_mate()), vec_copy(2, 1, me.x_mate()), vec_copy(3, 2, me.core_mate())
    for i in range(1, na):
        vec_at(i).start()

    @pl.when(a < nq)
    def _():
        for h in range(FINE):
            @pl.when(a + 1 < na)
            def _():
                chain_up(a, h).start()

            @pl.when(a > 0)
            def _():
                chain_down(a, h).start()

        for h in range(FINE // 2):
            x_copy(a, h, FINE).start()
            y_copy(a, h, FINE).start()

    @pl.when(a >= nq)
    def _():
        x_copy(a, 0, HALVES).start()
        y_copy(a, 0, HALVES).start()
        if relay:
            @pl.when(a > 0)
            def _():
                relay_down(a).start()
        else:
            @pl.loop(1, na)
            def _(d):
                @pl.when(d <= a)
                def _():
                    direct(a - d).start()

    def rest(copy):
        @pl.when(a < nq)
        def _():
            for h in range(FINE // 2, FINE):
                copy(a, h, FINE).start()

        @pl.when(a >= nq)
        def _():
            copy(a, 1, HALVES).start()

    total = widen(tile[...], mine)
    for i in range(1, na):
        vec_at(i).wait()
        total = total + widen(tiles_in[i], me.sid((a - i + na) % na, b, y, c))
    vin[1] = total
    v_y.start()
    rest(y_copy)
    pass_chain(0)
    v_y.wait()
    vin[2] = vin[1] + vtmp[0]
    v_x.start()
    rest(x_copy)
    pass_chain(1)
    v_x.wait()
    vin[3] = vin[2] + vtmp[1]
    v_core.start()
    pass_chain(2)
    v_core.wait()
    vec[...] = vin[3] + vtmp[2]

    @pl.when(a < nq)
    def _():
        for h in range(FINE):
            core(a, b, y, h, FINE).start()

    @pl.when(a >= nq)
    def _():
        for h in range(HALVES):
            core(a, b, y, h, HALVES).start()

    for h in range(3, FINE):
        pass_chain(h)

    @pl.when(a >= nq)
    def _():
        if relay:
            @pl.when(a + 1 < na)
            def _():
                relay_up(a).start()
        else:
            @pl.loop(1, na)
            def _(d):
                @pl.when(a + d < na)
                def _():
                    direct(a + d).start()

    if relay:
        take_at(1)

    @pl.when(a >= nq + 1)
    def _():
        pass_plane(a, HALVES)

    for a_ in range(nq):
        pass_plane(a_, FINE)

    if relay:
        first = 1 + (a == 1).astype(jnp.int32)
        second = 2 + ((a == 1) | (a == 2)).astype(jnp.int32)

        @pl.when(a == 0)
        def _():
            share(first)

    loads[2].wait()

    @pl.loop(0, SEQ // 256)
    def _(t):
        at = pl.ds(pl.multiple_of(t * 256, 256), 256)
        x = tokens[at, :]
        centred = x - jnp.mean(x, -1, keepdims=True)
        inverse = lax.rsqrt(jnp.mean(centred * centred, -1, keepdims=True) + EPS)
        n1[at, :] = (centred * inverse * vec[0:1, :] + vec[1:2, :]).astype(bf16)

    @pl.when(a == nq)
    def _():
        pass_plane(a, HALVES)

    if relay:
        take_at(-1)
    for a_ in range(nq):
        pass_diag(a_, FINE)
    if relay:
        take_at(2)
    for a_ in range(nq):
        partner(a_, FINE)
    fetch_q = pltpu.make_async_copy(whole.at[pl.ds(0, 3 * D)], wq, wq_sem)
    fetch_q.start()
    if relay:
        take_at(-2)

        @pl.when(a > 0)
        def _():
            share(first)

    def save(k, src, dst):
        return pltpu.make_async_copy(src, dst, save_sem.at[k])

    save(0, n1, n1_out).start()
    fetch_q.wait()

    def project(begin, row, scale):
        @pl.loop(begin, begin + 3)
        def _(j):
            at = pl.ds(pl.multiple_of(j * 256, 256), 256)
            r = dot(n1[...], wq[at, :], NT)
            if row is not None:
                cols = pl.ds(pl.multiple_of((j - begin) * 256, 256), 256)
                r = r + vec[row:row + 1, cols]
            r = r.astype(bf16)
            if scale is not None:
                r = r * jnp.asarray(scale, bf16)
            qkv[:, at] = r

    project(0, 2, 0.125)
    project(3, None, None)
    project(6, 3, None)
    save(1, qkv, qkv_out).start()

    lo = lax.broadcasted_iota(jnp.int32, (1, 128), 1) < 64
    zero = jnp.zeros((), bf16)

    def attend(i):
        q_at = pl.ds(pl.multiple_of(i * 128, 128), 128)
        k_at = pl.ds(pl.multiple_of(D + i * 128, 128), 128)
        v_at = pl.ds(pl.multiple_of(2 * D + i * 128, 128), 128)
        for qb in range(SEQ // QB):
            span = (qb + 1) * QB
            outs, sums = [], []
            for h in range(2):
                block = qkv[qb * QB:span, q_at]
                block = jnp.where(lo, block, zero) if h == 0 else jnp.where(lo, zero, block)
                s = dot(block, qkv[:span, k_at], NT)
                qi = lax.broadcasted_iota(jnp.int32, (QB, QB), 0)
                ki = lax.broadcasted_iota(jnp.int32, (QB, QB), 1)
                diag = jnp.where(ki <= qi, s[:, span - QB:], NEG)
                s = jnp.concatenate([s[:, :span - QB], diag], 1) if qb else diag
                m = jnp.max(s, 1, keepdims=True)
                p = jnp.exp(s - m)
                l = jnp.sum(p, 1, keepdims=True)
                outs.append(dot(p.astype(bf16), qkv[:span, v_at], NN) / l)
                sums.append(m + jnp.log(l))
            mixed[qb * QB:span, q_at] = jnp.where(lo, outs[0], outs[1]).astype(bf16)
            lc[qb * QB:span, :] = jnp.where(lo, sums[0], sums[1])
        t = jnp.transpose(lc[...], (1, 0))
        lse[i, 0:1, :] = t[0:1]
        lse[i, 1:2, :] = t[64:65]

    def own_diag():
        @pl.when(a >= nq)
        def _():
            pass_diag(a, HALVES)

    def third(act):
        @pl.when(a == 0)
        def _():
            act(3)

    def third_column(a_):
        take(a_)
        share(a_)

    steps = ()
    if relay:
        steps = (
            (0, own_diag),
            (1, lambda: pass_plane(first, HALVES)), (1, lambda: share(second)),
            (3, lambda: pass_diag(first, HALVES)), (3, lambda: third(third_column)),
            (4, lambda: pass_plane(second, HALVES)),
            (5, lambda: pass_diag(second, HALVES)),
        )

    @pl.loop(0, PAIRS)
    def _(i):
        attend(i)
        for k, act_now in steps:
            @pl.when(i == k)
            def _():
                act_now()

    save(2, mixed, mixed_out).start()
    if relay:
        partner(first, HALVES)

        @pl.when(a == 0)
        def _():
            partner(second, HALVES)

        @pl.when(a > 0)
        def _():
            partner(a, HALVES)
    else:
        own_diag()
        for k in range(1, na):
            for a_ in (a + k, a - k):
                @pl.when((a_ >= nq) & (a_ < na))
                def _():
                    take(a_)
                    share(a_)
                    pass_plane(a_, HALVES)
                    pass_diag(a_, HALVES)

        @pl.loop(nq, na)
        def _(a_):
            partner(a_, HALVES)

    def settle():
        if relay:
            third(lambda a_: pass_diag(a_, HALVES))
            third(lambda a_: partner(a_, HALVES))

            @pl.when(a > 0)
            def _():
                partner(second, HALVES)

    fetch_o = pltpu.make_async_copy(whole.at[pl.ds(3 * D, D)], w_out, wq_sem)
    fetch_o.start()
    BLOCKS = FF // 256
    shift = (a == na - 1).astype(jnp.int32) * 3 if relay else 0

    def weights_in(j):
        at = (j + shift) % BLOCKS * 256
        slot = j % 2
        return (
            pltpu.make_async_copy(whole.at[pl.ds(pl.multiple_of(4 * D + at, 256), 256)], wf.at[slot], w_sem.at[slot]),
            pltpu.make_async_copy(
                whole.at[pl.ds(pl.multiple_of(4 * D + FF + at, 256), 256)], wd.at[slot], w_sem.at[2 + slot]
            ),
        )

    for one in weights_in(0):
        one.start()
    loads[3].wait()
    fetch_o.wait()
    length = lengths[0]

    def alive(t):
        return lax.broadcasted_iota(jnp.int32, (256, 1), 0) + t * 256 < length

    @pl.loop(0, SEQ // 256)
    def _(t):
        at = pl.ds(pl.multiple_of(t * 256, 256), 256)
        x = tokens[at, :] + dot(mixed[at, :], w_out[...], NT) + vec[4:5, :]
        after[at, :] = x
        centred = x - jnp.mean(x, -1, keepdims=True)
        inverse = lax.rsqrt(jnp.mean(centred * centred, -1, keepdims=True) + EPS)
        n2[at, :] = (centred * inverse * vec[5:6, :] + vec[6:7, :]).astype(bf16)
        acc[at, :] = x + vec[7:8, :]
        top_low[at, :] = jnp.where(alive(t), cot[at, :], 0.0).astype(bf16)
        ngrad[at, :] = jnp.zeros((256, D), f32)

    if relay:
        third(lambda a_: pass_plane(a_, HALVES))

    def put_grad(k, slot, row):
        return pltpu.make_async_copy(
            stage.at[slot, k], ge.at[pl.ds(pl.multiple_of(row, 256), 256)], stage_sem.at[slot, k]
        )

    def put_both(j):
        at = (j + shift) % BLOCKS * 256
        return put_grad(0, j % 2, D + at), put_grad(1, j % 2, D + FF + at)

    @pl.loop(0, BLOCKS)
    def _(j):
        @pl.when(j == 2)
        def _():
            settle()

        @pl.when(j + 1 < BLOCKS)
        def _():
            for one in weights_in(j + 1):
                one.start()

        for one in weights_in(j):
            one.wait()
        slot = j % 2
        unit = (j + shift) % BLOCKS
        line, cols = 8 + unit // 3, pl.ds(pl.multiple_of(unit % 3 * 256, 256), 256)
        bias = vec[pl.ds(line, 1), cols]
        sums = jnp.zeros((1, 256), f32)
        for t in range(SEQ // 256):
            at = pl.ds(t * 256, 256)
            x = dot(n2[at, :], wf[slot], NT) + bias
            g = dot(top_low[at, :], wd[slot], NT)
            square = x * x
            part = 0.5 + 0.5 * jnp.tanh(ROOT * x * (1.0 + CUBIC * square))
            active = (x * part).astype(bf16)
            slope = part * (1.0 + (2.0 * ROOT) * x * (1.0 - part) * (1.0 + (3.0 * CUBIC) * square))
            g = g * slope
            sums = sums + jnp.sum(g, 0, keepdims=True)
            g = g.astype(bf16)
            act[at, :] = active
            hid[at, :] = g
            acc[at, :] += dot(active, wd[slot], NN)
            ngrad[at, :] += dot(g, wf[slot], NN)
        part_sums[pl.ds(line, 1), cols] = sums

        @pl.when(j >= 2)
        def _():
            for one in put_both(j - 2):
                one.wait()

        stage[slot, 0] = dot(hid[...], n2[...], TN).astype(bf16)
        stage[slot, 1] = dot(act[...], top_low[...], TN).astype(bf16)
        for one in put_both(j):
            one.start()

    part_sums[0:8, :] = jnp.zeros((8, D), f32)
    part_sums[12:16, :] = jnp.zeros((4, D), f32)

    @pl.loop(0, SEQ // 256)
    def _(t):
        at = pl.ds(pl.multiple_of(t * 256, 256), 256)
        live = alive(t)
        x = after[at, :]
        centred = x - jnp.mean(x, -1, keepdims=True)
        inverse = lax.rsqrt(jnp.mean(centred * centred, -1, keepdims=True) + EPS)
        unit = centred * inverse
        g = ngrad[at, :]
        e = g * vec[5:6, :]
        top = jnp.where(live, cot[at, :], 0.0)
        mid = top + inverse * (e - jnp.mean(e, -1, keepdims=True) - unit * jnp.mean(e * unit, -1, keepdims=True))
        low[at, :] = mid.astype(bf16)
        part_sums[4:5, :] += jnp.sum(mid, 0, keepdims=True)
        part_sums[5:6, :] += jnp.sum(g * unit, 0, keepdims=True)
        part_sums[6:7, :] += jnp.sum(g, 0, keepdims=True)
        part_sums[7:8, :] += jnp.sum(top, 0, keepdims=True)
        ngrad[at, :] = mid + jnp.where(live, 0.0, cot[at, :])
        acc[at, :] = jnp.where(live, acc[at, :], tokens[at, :])

    finals = [save(3, low, low_out), save(4, ngrad, base_out), save(5, acc, block_out)]
    for one in finals:
        one.start()
    for j in (BLOCKS - 2, BLOCKS - 1):
        for one in put_both(j):
            one.wait()

    @pl.loop(0, 3)
    def _(j):
        @pl.when(j >= 2)
        def _():
            put_grad(0, 0, 0).wait()

        stage[j % 2, 0] = dot(low[:, pl.ds(pl.multiple_of(j * 256, 256), 256)], mixed[...], TN).astype(bf16)
        put_grad(0, j % 2, j * 256).start()

    put_grad(0, 1, 256).wait()
    put_grad(0, 0, 512).wait()
    for one in [save(0, n1, n1_out), save(1, qkv, qkv_out), save(2, mixed, mixed_out)] + finals:
        one.wait()

    def sent(a_, n):
        for h in range(n):
            x_copy(a_, h, n).wait_send()
            y_copy(a_, h, n).wait_send()
            diag_send(a_, h, n).wait_send()
            for b_, y_ in around:
                core(a_, b_, y_, h, n).wait_send()

    for a_ in range(nq):
        sent(a_, FINE)
        for h in range(FINE):
            @pl.when((a_ <= a) & (a + 1 < na))
            def _():
                chain_up(a_, h).wait_send()

            @pl.when((a_ >= a) & (a > 0))
            def _():
                chain_down(a_, h).wait_send()

    @pl.loop(nq, na)
    def _(a_):
        sent(a_, HALVES)

    if relay:
        @pl.loop(nq, na)
        def _(a_):
            @pl.when((a_ <= a) & (a + 1 < na))
            def _():
                relay_up(a_).wait_send()

            @pl.when((a_ >= a) & (a > 0))
            def _():
                relay_down(a_).wait_send()
    else:
        @pl.when(a >= nq)
        def _():
            @pl.loop(0, na)
            def _(to):
                @pl.when(to != a)
                def _():
                    direct(to).wait_send()


def forward(n_dp, lengths, tokens, master, vector, cotangent):
    na = n_dp // 2
    rows = master.shape[0]
    count = na * 8
    dma = pltpu.SemaphoreType.DMA
    vm, hbm = pl.BlockSpec(memory_space=pltpu.VMEM), pl.BlockSpec(memory_space=pl.ANY)
    wide, full = pltpu.VMEM((SEQ, D), f32), pltpu.VMEM((SEQ, D), bf16)
    block = pltpu.VMEM((2, 256, D), bf16)

    def out(rows, dtype, columns=D):
        return jax.ShapeDtypeStruct((rows, columns), dtype)

    return pl.pallas_call(
        functools.partial(forward_kernel, n_dp),
        in_specs=[pl.BlockSpec(memory_space=pltpu.SMEM), hbm, hbm, hbm, hbm],
        out_specs=[hbm] * 8 + [vm, vm, vm],
        out_shape=[
            out(count * rows, bf16), out(count * rows - 3 * D, bf16), out(SEQ, bf16), out(SEQ, bf16, 3 * D),
            out(SEQ, bf16), out(SEQ, bf16), out(SEQ, f32), out(SEQ, f32), out(16, f32),
            jax.ShapeDtypeStruct((PAIRS, 8, SEQ), f32), out(16, f32),
        ],
        scratch_shapes=[
            wide, pltpu.VMEM((rows, D), f32), pltpu.VMEM(vector.shape, f32), wide, dma((4,)), dma((6,)),
            full, pltpu.VMEM((SEQ, 3 * D), bf16), full, full, wide, wide, wide, full, full,
            pltpu.VMEM((SEQ, 256), bf16), pltpu.VMEM((SEQ, 256), bf16), pltpu.VMEM((D, D), bf16),
            block, block, dma((4,)), pltpu.VMEM((2, 2, 256, D), bf16), dma((2, 2)),
            pltpu.VMEM((rows, D), bf16), dma,
            pltpu.VMEM((3 * D, D), bf16), dma,
            pltpu.VMEM((16, 128), f32), pltpu.VMEM((na, 16, 128), f32),
            pltpu.VMEM((4, 16, D), f32), pltpu.VMEM((3, 16, D), f32), dma((3 + na,)), dma((3 + na,)),
            pltpu.VMEM((SEQ, 128), f32),
            dma((2 * na, FINE)), dma((na, FINE)), dma((na,)), dma((na,)), dma((na,)),
            dma((na, FINE)), dma((na, FINE)),
            dma((na, FINE)), dma((na, FINE)),
            dma((na, FINE)), dma((na, FINE)),
            dma((na, 4, FINE)), dma((na, 4, FINE)),
        ],
        compiler_params=pltpu.CompilerParams(
            collective_id=1, has_side_effects=True, vmem_limit_bytes=66_000_000
        ),
        name="gather_forward",
    )(lengths, tokens, master, vector, cotangent)


def tiles(rows, parts):
    marks = [16 * round(rows * h / parts / 16) for h in range(parts)] + [rows]
    return [(marks[h], marks[h + 1] - marks[h]) for h in range(parts)]


def backward_kernel(
    n_dp, weights, ge, qkv_in, mixed_in, lse, n1_in, low_in, tokens_in, base_in, vec, part,
    gl, out, total, vector_total,
    w_out, w_qkv, qkv, mixed, n1, low, tokens, base, load_sem,
    do, proj, stage, stage_sem, kT, dqT, dk_s, dv_s, dl,
    gbuf, kbuf, dbuf, xbuf, ybuf, zbuf, cbuf, vin, vtmp,
    ls, ks, kr, ds, dr, xs, xr, ys, yr, zs, zr, cs, cr, vs, vr,
):
    me = Place(n_dp)
    na = me.na
    nq = na // 4
    a, b, y, c = me.a, me.b, me.y, me.c
    rows = total.shape[0]
    around = ((b, y), (1 - b, y), (b, 1 - y), (1 - b, 1 - y))
    quarters = tiles(rows, 4)
    early = 3 * D

    def span(q):
        return quarters[2 * q][0], quarters[2 * q][1] + quarters[2 * q + 1][1]

    def grads(a_, o, core, q):
        first, size = span(q)
        at = me.sid(a_, *around[o], core) * rows + first
        if isinstance(a_, int):
            return gl.at[pl.ds(pl.multiple_of(at, 8), size)]
        return ge.at[pl.ds(pl.multiple_of(at - early, 8), size)]

    def fetch(a_, o, q):
        return pltpu.make_async_copy(grads(a_, o, c, q), gbuf.at[a_, o, pl.ds(*span(q))], ls.at[a_, o, q])

    def to_core(a_, o, q):
        return pltpu.make_async_remote_copy(
            src_ref=grads(a_, o, 1 - c, q), dst_ref=kbuf.at[a_, o, pl.ds(*span(q))],
            send_sem=ks.at[a_, o, q], recv_sem=kr.at[a_, o, q], device_id=me.core_mate(),
        )

    def move(src, dst, send, recv, peer):
        return pltpu.make_async_remote_copy(src_ref=src, dst_ref=dst, send_sem=send, recv_sem=recv, device_id=peer)

    def diag(a_, h):
        at = pl.ds(*quarters[h])
        peer = me.x_mate() if h % 2 == 0 else me.y_mate()
        return move(kbuf.at[a_, 3, at], dbuf.at[a_, at], ds.at[a_, h], dr.at[a_, h], peer)

    def x_copy(a_, h):
        at = pl.ds(*quarters[h])
        return move(kbuf.at[a_, 1, at], xbuf.at[a_, at], xs.at[a_, h], xr.at[a_, h], me.x_mate())

    def y_copy(a_, h):
        at = pl.ds(*quarters[h])
        return move(kbuf.at[a_, 2, at], ybuf.at[a_, at], ys.at[a_, h], yr.at[a_, h], me.y_mate())

    def direct(a_, q):
        at = pl.ds(*span(q))
        return move(kbuf.at[a_, 0, at], zbuf.at[a, at], zs.at[a_, q], zr.at[a, q], me.at(a_))

    def direct_from(a_, q):
        at = pl.ds(*span(q))
        return move(kbuf.at[a_, 0, at], zbuf.at[a_, at], zs.at[a_, q], zr.at[a_, q], me.at(a_))

    def chain(a_, h, down):
        at = pl.ds(*quarters[h])
        way = 0 if down else 1
        return move(
            kbuf.at[a_, 0, at], cbuf.at[a_, way, at], cs.at[a_, h], cr.at[a_, way, h], me.at(a - 1 if down else a + 1)
        )

    def add(to, frm):
        kbuf[to] = (kbuf[to].astype(f32) + frm.astype(f32)).astype(bf16)

    def start(a_, q):
        for o in range(4):
            to_core(a_, o, q).start()
            fetch(a_, o, q).start()

    def pair_sum(a_, q):
        at = pl.ds(*span(q))
        for o in (3, 1, 2, 0):
            to_core(a_, o, q).wait_recv()
            fetch(a_, o, q).wait()
            add((a_, o, at), gbuf[a_, o, at])
            if o == 3:
                diag(a_, 2 * q).start()
                diag(a_, 2 * q + 1).start()
            if o == 1:
                x_copy(a_, 2 * q).start()
            if o == 2:
                y_copy(a_, 2 * q + 1).start()

    def diag_sum(a_, q):
        at = pl.ds(*quarters[2 * q])
        diag(a_, 2 * q).wait_recv()
        add((a_, 2, at), dbuf[a_, at])
        y_copy(a_, 2 * q).start()
        at = pl.ds(*quarters[2 * q + 1])
        diag(a_, 2 * q + 1).wait_recv()
        add((a_, 1, at), dbuf[a_, at])
        x_copy(a_, 2 * q + 1).start()

    def plane_sum(a_, h):
        at = pl.ds(*quarters[h])
        x_copy(a_, h).wait_recv()
        y_copy(a_, h).wait_recv()
        add((a_, 0, at), xbuf[a_, at].astype(f32) + ybuf[a_, at].astype(f32))

    def spread(a_, q):
        plane_sum(a_, 2 * q)
        plane_sum(a_, 2 * q + 1)

        @pl.when(a_ != a)
        def _():
            direct(a_, q).start()

    def link(a_, h):
        at = pl.ds(*quarters[h])
        plane_sum(a_, h)

        @pl.when(a > a_)
        def _():
            @pl.when(a + 1 < na)
            def _():
                chain(a_, h, True).wait_recv()
                add((a_, 0, at), cbuf[a_, 0, at])

            chain(a_, h, True).start()

        @pl.when(a < a_)
        def _():
            @pl.when(a > 0)
            def _():
                chain(a_, h, False).wait_recv()
                add((a_, 0, at), cbuf[a_, 1, at])

            chain(a_, h, False).start()

    def item(i):
        return nq + i // 2 + 0 * a, i % 2

    def local(k, src, dst):
        return pltpu.make_async_copy(src, dst, load_sem.at[k])

    loads = [
        local(0, low_in, low), local(1, weights.at[pl.ds(3 * D, D)], w_out), local(2, qkv_in, qkv),
        local(3, mixed_in, mixed), local(4, n1_in, n1), local(5, weights.at[pl.ds(0, 3 * D)], w_qkv),
        local(6, tokens_in, tokens), local(7, base_in, base),
    ]
    for load in loads[:4]:
        load.start()
    greet(me)

    @pl.loop(nq, na)
    def _(a_):
        for q in range(2):
            start(a_, q)

    for load in loads[4:]:
        load.start()
    loads[0].wait()
    loads[1].wait()

    @pl.loop(0, 3)
    def _(j):
        at = pl.ds(pl.multiple_of(j * 256, 256), 256)
        do[:, at] = dot(low[...], w_out[:, at], NN).astype(bf16)

    pair_sum(*item(0))
    pair_sum(*item(1))
    loads[2].wait()
    loads[3].wait()

    lo = lax.broadcasted_iota(jnp.int32, (1, 128), 1) < 64
    zero = jnp.zeros((), bf16)

    def attend_back(i):
        q_at = pl.ds(pl.multiple_of(i * 128, 128), 128)
        k_at = pl.ds(pl.multiple_of(D + i * 128, 128), 128)
        v_at = pl.ds(pl.multiple_of(2 * D + i * 128, 128), 128)
        prod = do[:, q_at].astype(f32) * mixed[:, q_at].astype(f32)
        d0 = jnp.sum(jnp.where(lo, prod, 0.0), 1, keepdims=True)
        d1 = jnp.sum(jnp.where(lo, 0.0, prod), 1, keepdims=True)
        dl[...] = jnp.transpose(jnp.where(lo, d0, d1), (1, 0))
        kT[...] = jnp.transpose(qkv[:, k_at], (1, 0))
        for qb in range(SEQ // QB):
            q0 = qb * QB
            end = q0 + QB
            for h in range(2):
                offset = lse[i, h:h + 1, q0:end]
                delta = dl[64 * h:64 * h + 1, q0:end]
                qm, dm = qkv[q0:end, q_at], do[q0:end, q_at]
                qm = jnp.where(lo, qm, zero) if h == 0 else jnp.where(lo, zero, qm)
                dm = jnp.where(lo, dm, zero) if h == 0 else jnp.where(lo, zero, dm)
                s = dot(qkv[:end, k_at], qm, NT)
                ki = lax.broadcasted_iota(jnp.int32, (QB, QB), 0)
                qi = lax.broadcasted_iota(jnp.int32, (QB, QB), 1)
                last = jnp.where(ki <= qi, s[q0:], NEG)
                s = jnp.concatenate([s[:q0], last], 0) if qb else last
                p = jnp.exp(s - offset)
                dp = dot(qkv[:end, v_at], dm, NT)
                dsc = (p * (dp - delta)).astype(bf16)
                pv = dot(p.astype(bf16), dm, NN)
                pk = dot(dsc, qm, NN)
                if h == 0:
                    if qb:
                        dv_s[:q0, :] += pv[:q0]
                        dk_s[:q0, :] += pk[:q0]
                    dv_s[q0:end, :] = pv[q0:]
                    dk_s[q0:end, :] = pk[q0:]
                else:
                    dv_s[:end, :] += pv
                    dk_s[:end, :] += pk
                dqT[64 * h:64 * h + 64, q0:end] = dot(kT[64 * h:64 * h + 64, :end], dsc, NN)
        dq = jnp.transpose(dqT[...], (1, 0)) * 0.125
        dv = dv_s[...]
        proj[:, q_at] = dq.astype(bf16)
        proj[:, k_at] = dk_s[...].astype(bf16)
        proj[:, v_at] = dv.astype(bf16)
        vin[0, 2:3, q_at] = jnp.sum(dq, 0, keepdims=True)
        vin[0, 3:4, q_at] = jnp.sum(dv, 0, keepdims=True)

    vin[0] = part[...]
    steps = ((0, diag_sum, 0), (1, pair_sum, 2), (1, diag_sum, 1), (2, spread, 0), (2, pair_sum, 3),
             (3, diag_sum, 2), (3, spread, 1), (4, diag_sum, 3), (5, spread, 2), (5, pair_sum, 4))

    @pl.loop(0, PAIRS)
    def _(i):
        attend_back(i)
        for k, act, which in steps:
            @pl.when(i == k)
            def _():
                act(*item(which))

    loads[4].wait()

    def save(j):
        return pltpu.make_async_copy(
            stage.at[j % 2], gl.at[pl.ds(pl.multiple_of(j * 256, 256), 256)], stage_sem.at[j % 2]
        )

    @pl.loop(0, 9)
    def _(j):
        @pl.when(j >= 2)
        def _():
            save(j - 2).wait()

        stage[j % 2] = dot(proj[:, pl.ds(pl.multiple_of(j * 256, 256), 256)], n1[...], TN).astype(bf16)
        save(j).start()

    save(7).wait()
    save(8).wait()
    for a_ in range(nq):
        for q in range(2):
            start(a_, q)
    for load in loads[5:]:
        load.wait()

    def norm_back(t):
        at = pl.ds(t * 256, 256)
        x = tokens[at, :]
        centred = x - jnp.mean(x, -1, keepdims=True)
        inverse = lax.rsqrt(jnp.mean(centred * centred, -1, keepdims=True) + EPS)
        unit = centred * inverse
        g = dot(proj[at, :], w_qkv[...], NN)
        e = g * vec[0:1, :]
        out[at, :] = base[at, :] + inverse * (
            e - jnp.mean(e, -1, keepdims=True) - unit * jnp.mean(e * unit, -1, keepdims=True)
        )
        vin[0, 0:1, :] += jnp.sum(g * unit, 0, keepdims=True)
        vin[0, 1:2, :] += jnp.sum(g, 0, keepdims=True)

    def after(t):
        if t == 0:
            for a_ in range(nq):
                for q in range(2):
                    pair_sum(a_, q)
        if t == 1:
            diag_sum(*item(4))
            spread(*item(3))
        if t == 2:
            for a_ in range(nq):
                diag_sum(a_, 0)
                diag_sum(a_, 1)
            pair_sum(*item(5))
        if t == 3:
            spread(*item(4))

    for t in range(4):
        norm_back(t)
        after(t)

    def vec_copy(i, k, peer):
        return pltpu.make_async_remote_copy(
            src_ref=vin.at[i], dst_ref=vtmp.at[k], send_sem=vs.at[k], recv_sem=vr.at[k], device_id=peer
        )

    v_core, v_y, v_x = vec_copy(0, 0, me.core_mate()), vec_copy(1, 1, me.y_mate()), vec_copy(2, 2, me.x_mate())

    def vec_at(i):
        return vec_copy(3, 2 + i, me.at((a + i) % na))

    v_core.start()
    diag_sum(*item(5))
    v_core.wait()
    vin[1] = vin[0] + vtmp[0]
    v_y.start()
    for a_ in range(nq):
        link(a_, 0)
        link(a_, 1)
    v_y.wait()
    vin[2] = vin[1] + vtmp[1]
    v_x.start()
    for a_ in range(nq):
        link(a_, 2)
        link(a_, 3)
    v_x.wait()
    vin[3] = vin[2] + vtmp[2]
    for i in range(1, na):
        vec_at(i).start()
    spread(*item(5))

    if na > 4:
        @pl.loop(nq + 3, na)
        def _(a_):
            for q in range(2):
                pair_sum(a_, q)
                diag_sum(a_, q)
                spread(a_, q)

    vsum = vin[3]
    for i in range(1, na):
        vec_at(i).wait()
        vsum = vsum + vtmp[2 + i]
    vector_total[...] = vsum

    @pl.when(a >= nq)
    def _():
        total[...] = kbuf[a, 0].astype(f32)

        @pl.loop(1, na)
        def _(i):
            frm = (a + i) % na
            for q in range(2):
                direct_from(frm, q).wait_recv()
            total[...] += zbuf[frm].astype(f32)

    for a_ in range(nq):
        @pl.when(a == a_)
        def _():
            total[...] = kbuf[a_, 0].astype(f32)

            @pl.when(a + 1 < na)
            def _():
                for h in range(4):
                    chain(a_, h, True).wait_recv()
                total[...] += cbuf[a_, 0].astype(f32)

            @pl.when(a > 0)
            def _():
                for h in range(4):
                    chain(a_, h, False).wait_recv()
                total[...] += cbuf[a_, 1].astype(f32)

        @pl.when(a != a_)
        def _():
            for h in range(4):
                chain(a_, h, True).wait_send()

    def sent(a_):
        for q in range(2):
            for o in range(4):
                to_core(a_, o, q).wait_send()
        for h in range(4):
            diag(a_, h).wait_send()
            x_copy(a_, h).wait_send()
            y_copy(a_, h).wait_send()

    for a_ in range(nq):
        sent(a_)

    @pl.loop(nq, na)
    def _(a_):
        sent(a_)

        @pl.when(a_ != a)
        def _():
            for q in range(2):
                direct(a_, q).wait_send()


def backward(n_dp, rows, weights, ge, qkv, mixed, lse, n1, low, tokens, base, vec, part):
    na = n_dp // 2
    nq = na // 4
    dma = pltpu.SemaphoreType.DMA
    vm, anyw = pl.BlockSpec(memory_space=pltpu.VMEM), pl.BlockSpec(memory_space=pl.ANY)
    full = pltpu.VMEM((SEQ, D), bf16)
    wide = pltpu.VMEM((SEQ, D), f32)
    return pl.pallas_call(
        functools.partial(backward_kernel, n_dp),
        in_specs=[anyw, anyw, anyw, anyw, vm, anyw, anyw, anyw, anyw, vm, vm],
        out_specs=[anyw, vm, vm, vm],
        out_shape=[
            jax.ShapeDtypeStruct((3 * D, D), bf16),
            jax.ShapeDtypeStruct((SEQ, D), f32),
            jax.ShapeDtypeStruct((rows, D), f32),
            jax.ShapeDtypeStruct((16, D), f32),
        ],
        scratch_shapes=[
            pltpu.VMEM((D, D), bf16), pltpu.VMEM((3 * D, D), bf16), pltpu.VMEM((SEQ, 3 * D), bf16),
            full, full, full, wide, wide, dma((8,)),
            full, pltpu.VMEM((SEQ, 3 * D), bf16), pltpu.VMEM((2, 256, D), bf16), dma((2,)),
            pltpu.VMEM((128, SEQ), bf16), pltpu.VMEM((128, SEQ), f32),
            pltpu.VMEM((SEQ, 128), f32), pltpu.VMEM((SEQ, 128), f32), pltpu.VMEM((128, SEQ), f32),
            pltpu.VMEM((na, 4, rows, D), bf16), pltpu.VMEM((na, 4, rows, D), bf16),
            pltpu.VMEM((na, rows, D), bf16), pltpu.VMEM((na, rows, D), bf16),
            pltpu.VMEM((na, rows, D), bf16), pltpu.VMEM((na, rows, D), bf16),
            pltpu.VMEM((nq, 2, rows, D), bf16),
            pltpu.VMEM((4, 16, D), f32), pltpu.VMEM((2 + na, 16, D), f32),
            dma((na, 4, 2)), dma((na, 4, 2)), dma((na, 4, 2)),
            dma((na, 4)), dma((na, 4)), dma((na, 4)), dma((na, 4)), dma((na, 4)), dma((na, 4)),
            dma((na, 2)), dma((na, 2)), dma((nq, 4)), dma((nq, 2, 4)), dma((2 + na,)), dma((2 + na,)),
        ],
        compiler_params=pltpu.CompilerParams(
            collective_id=2, has_side_effects=True, vmem_limit_bytes=66_000_000
        ),
        name="attend_reduce",
    )(weights, ge, qkv, mixed, lse, n1, low, tokens, base, vec, part)


BETA_ONE = 0.9
BETA_TWO = 0.95
ADAM_EPS = 1e-08
ADAM_STEP = 2
LR_MATRIX = 0.05
LR_VECTOR = 0.1
DECAY = 0.1
GRAD_FACTOR = 4.0


def adamw(master, gradient, moment, square, rate, decay):
    moment_new = BETA_ONE * moment + (1.0 - BETA_ONE) * gradient
    square_new = BETA_TWO * square + (1.0 - BETA_TWO) * gradient * gradient
    first_fix = 1.0 - BETA_ONE**ADAM_STEP
    second_fix = 1.0 - BETA_TWO**ADAM_STEP
    stride = moment_new / first_fix / (jnp.sqrt(square_new / second_fix) + ADAM_EPS)
    return (master - rate * (stride + decay * master), moment_new, square_new)


def body(
    tokens, cotangent, lengths, master_matrix, master_vector,
    moment_matrix, moment_vector, square_matrix, square_vector,
):
    n_dp, n_zero = lax.axis_size("dp"), lax.axis_size("zero")
    weights, early, normed_one, qkv, mixed, mid_low, base, block_out, vectors, lse, part = forward(
        n_dp, lengths, tokens, master_matrix, master_vector, cotangent
    )
    late, input_gradient, matrix_total, vector_sum = backward(
        n_dp, master_matrix.shape[0], weights, early, qkv, mixed, lse, normed_one, mid_low, tokens, base, vectors, part
    )
    columns = master_vector.shape[1]
    mine = (lax.axis_index("dp") * n_zero + lax.axis_index("zero")) * columns
    vector_total = lax.dynamic_slice(vector_sum, (0, mine), (12, columns))
    scale = GRAD_FACTOR * float(SEQ * n_dp * n_zero) ** (-0.5)
    matrix_gradient = matrix_total * scale
    vector_gradient = vector_total * scale
    matrix_weights, matrix_moment, matrix_square = adamw(
        master_matrix, matrix_gradient, moment_matrix, square_matrix, LR_MATRIX, DECAY
    )
    vector_weights, vector_moment, vector_square = adamw(
        master_vector, vector_gradient, moment_vector, square_vector, LR_VECTOR, 0.0
    )
    return (
        block_out, input_gradient, matrix_gradient, vector_gradient, matrix_weights,
        vector_weights, matrix_moment, vector_moment, matrix_square, vector_square,
    )


def solution(mesh):
    rows, columns = P(("dp", "zero"), None), P(None, ("dp", "zero"))
    return jax.shard_map(
        body,
        mesh=mesh,
        in_specs=(rows, rows, P(("dp", "zero")), rows, columns, rows, columns, rows, columns),
        out_specs=(rows, rows, rows, columns, rows, columns, rows, columns, rows, columns),
        check_vma=False,
    )
```

profile of v0, /device:TPU:0, one launch (start us, length us, event | category | flops | bytes accessed | tf_op | source)
XLA Modules:
  0.0 251.7 jit_solution(15376632612706263785)
XLA Ops:
  1.3 140.8 %gather_forward.1 = (bf16[9216,768]{1,0:T(8,128)(2,1)}, bf16[6912,768]{1,0:T(8,128)(2,1)}, bf16[1024,768]{1,0:T(8,128)(2,1)}, bf16[1024,2304]{1,0:T(8,128)(2,1)}...) custom-call(s32[1]{0:T(128)S(6)} %copy.21.lengths, ...), custom_call_target="tpu_custom_call" | custom-call | tf_op jit(solution)/shard_map/gather_forward/pallas_call | solution.py:685
  142.1 0.0 copy-start
  142.1 98.4 %attend_reduce.1 = (bf16[2304,768]{1,0:T(8,128)(2,1)}, f32[1024,768]{1,0:T(8,128)}, f32[288,768]{1,0:T(8,128)}, f32[16,768]{1,0:T(8,128)}) custom-call(bf16[9216,768]{1,0:T(8,128)(2,1)} %get-tuple-element.25.weights, bf16[6912,768]{1,0:T(8,128)(2,1)} %get-tuple-element.26.ge, bf16[1024,2304]{1,0:T(8,128)(2,1)} %get-tuple-element.27.qkv_in, ...), custom_call_target="tpu_custom_call" | custom-call | tf_op jit(solution)/shard_map/attend_reduce/pallas_call | solution.py:1117
  240.5 0.0 copy-done
  240.6 0.0 copy-start.2
  240.6 0.0 copy-start.3
  240.6 0.0 copy-start.4
  240.6 4.1 %multiply_subtract_fusion = (f32[288,768]{1,0:T(8,128)}, f32[288,768]{1,0:T(8,128)}, f32[288,768]{1,0:T(8,128)}, f32[288,768]{1,0:T(8,128)}) fusion(f32[288,768]{1,0:T(8,128)S(1)} %copy-done, f32[288,768]{1,0:T(8,128)} %get-tuple-element.36, f32[288,768]{1,0:T(8,128)} %param.14, f32[288,768]{1,0:T(8,128)} %param.16), kind=kLoop, calls=%fused_computation | loop fusion | flops 3538944 | bytes 7077888 | tf_op jit(solution)/shard_map/sub | solution.py:1165
  244.6 0.0 copy-done.2
  244.6 0.0 copy-done.3
  244.6 0.0 copy-done.4
  244.7 1.4 multiply_subtract_fusion.1
  246.1 0.0 copy-start.1
  246.1 3.9 %copy.22 = f32[1024,768]{1,0:T(8,128)} copy(f32[1024,768]{1,0:T(8,128)} %get-tuple-element.56) | data formatting | bytes 6291456
  250.0 0.0 copy-done.1
  250.0 1.7 copy.23
Async XLA Ops:
  142.1 98.4 %copy-start = (f32[288,768]{1,0:T(8,128)S(1)}, f32[288,768]{1,0:T(8,128)}, u32[]{:S(2)}) copy-start(f32[288,768]{1,0:T(8,128)} %master_in.1) | copy-start | bytes 2654212
  240.6 4.1 %copy-start.2 = (f32[12,24]{1,0:T(8,128)S(1)}, f32[12,24]{1,0:T(8,128)}, u32[]{:S(2)}) copy-start(f32[12,24]{1,0:T(8,128)} %vector_in.1) | copy-start | bytes 3460
  240.6 4.1 %copy-start.3 = (f32[12,24]{1,0:T(8,128)S(1)}, f32[12,24]{1,0:T(8,128)}, u32[]{:S(2)}) copy-start(f32[12,24]{1,0:T(8,128)} %param.15) | copy-start | bytes 3460
  240.6 4.1 %copy-start.4 = (f32[12,24]{1,0:T(8,128)S(1)}, f32[12,24]{1,0:T(8,128)}, u32[]{:S(2)}) copy-start(f32[12,24]{1,0:T(8,128)} %param.17) | copy-start | bytes 3460
  246.1 3.9 %copy-start.1 = (f32[1024,768]{1,0:T(8,128)S(1)}, f32[1024,768]{1,0:T(8,128)}, u32[]{:S(2)}) copy-start(f32[1024,768]{1,0:T(8,128)} %get-tuple-element.57) | copy-start | bytes 9437188
where the time goes:
time: 252 us
  Pallas kernels  239 us (95%)
  local copies, waits for them, and re-layouts  5.6 us (2%)
  other arithmetic  5.48 us (2%)
    pallas_call x1, Pallas kernels, forward(): pl.pallas_call(functools.partial(forward_kernel, n_dp), in_specs=[pl.Bloc...  141 us
    pallas_call x1, Pallas kernels, backward(): pl.pallas_call(functools.partial(backward_kernel, n_dp), in_specs=[anyw,...  98.4 us
    unnamed x12, local copies, waits for them, and re-layouts  5.6 us
    sub x2, other arithmetic, adamw(): return (master - rate * (stride + decay * master), moment_new, square_new)  5.48 us

commit v1 on v0

--- a/solution.py
+++ b/solution.py
@@ -50,17 +50,22 @@
     def core_mate(self):
         return self.dev(self.a, self.b, self.y, 1 - self.c)
 
+    def plane_mate(self, r):
+        b = 1 - self.b if r & 1 else self.b
+        y = 1 - self.y if r & 2 else self.y
+        return self.dev(self.a, b, y, 1 - self.c if r & 4 else self.c)
+
     def at(self, a):
         return self.dev(a, self.b, self.y, self.c)
 
 
-def greet(me):
+def greet(me, peers):
     barrier = pltpu.get_barrier_semaphore()
-    for peer in (me.x_mate(), me.y_mate(), me.core_mate()):
+    for peer in peers:
         pl.semaphore_signal(barrier, inc=1, device_id=peer)
     for i in range(1, me.na):
         pl.semaphore_signal(barrier, inc=1, device_id=me.at((me.a + i) % me.na))
-    pl.semaphore_wait(barrier, me.na + 2)
+    pl.semaphore_wait(barrier, me.na - 1 + len(peers))
 
 
 FINE = 4
@@ -160,13 +165,6 @@
             def _():
                 relay_down(a_).start()
 
-    def take_at(k):
-        a_ = a + k
-
-        @pl.when((a_ >= nq) & (a_ < na))
-        def _():
-            take(a_)
-
     def share(a_):
         for h in range(HALVES):
             column_sends(a_, h, HALVES)
@@ -217,21 +215,21 @@
         ) & (lax.broadcasted_iota(jnp.int32, (128, D), 0) < columns)
         return dot(small.astype(bf16), move.astype(bf16), NN)
 
-    greet(me)
+    greet(me, [me.plane_mate(r) for r in range(1, 8)])
     put.wait()
 
-    def vec_copy(i, k, peer):
+    def vec_copy(r):
         return pltpu.make_async_remote_copy(
-            src_ref=vin.at[i], dst_ref=vtmp.at[k], send_sem=vs_sem.at[k], recv_sem=vr_sem.at[k], device_id=peer
+            src_ref=vin, dst_ref=vtmp.at[r], send_sem=vs_sem.at[r], recv_sem=vr_sem.at[r],
+            device_id=me.plane_mate(r),
         )
 
     def vec_at(i):
         return pltpu.make_async_remote_copy(
-            src_ref=tile, dst_ref=tiles_in.at[i], send_sem=vs_sem.at[2 + i], recv_sem=vr_sem.at[2 + i],
+            src_ref=tile, dst_ref=tiles_in.at[i], send_sem=vs_sem.at[7 + i], recv_sem=vr_sem.at[7 + i],
             device_id=me.at((a + i) % na),
         )
 
-    v_y, v_x, v_core = vec_copy(1, 0, me.y_mate()), vec_copy(2, 1, me.x_mate()), vec_copy(3, 2, me.core_mate())
     for i in range(1, na):
         vec_at(i).start()
 
@@ -265,35 +263,76 @@
                 def _():
                     direct(a - d).start()
 
-    def rest(copy):
-        @pl.when(a < nq)
-        def _():
-            for h in range(FINE // 2, FINE):
-                copy(a, h, FINE).start()
-
-        @pl.when(a >= nq)
-        def _():
+    def rest():
+        for copy in (x_copy, y_copy):
             copy(a, 1, HALVES).start()
 
     total = widen(tile[...], mine)
     for i in range(1, na):
         vec_at(i).wait()
         total = total + widen(tiles_in[i], me.sid((a - i + na) % na, b, y, c))
-    vin[1] = total
-    v_y.start()
-    rest(y_copy)
+    vin[...] = total.astype(bf16)
+    for r in range(1, 8):
+        vec_copy(r).start()
+
+    @pl.when(a < nq)
+    def _():
+        for h in range(FINE // 2, FINE):
+            x_copy(a, h, FINE).start()
+            y_copy(a, h, FINE).start()
+
+    @pl.when(a > nq if relay else a >= nq)
+    def _():
+        rest()
+
+    def at_slot(slot):
+        for k in range(na if relay else 0):
+            acts = plan[k].get(slot, ())
+
+            if acts:
+                @pl.when(a == k)
+                def _():
+                    for act_now, plane in acts:
+                        act_now(plane)
+
+    def plane(a_):
+        pass_plane(a_, HALVES)
+
+    def diagonal(a_):
+        pass_diag(a_, HALVES)
+
+    def partners(a_):
+        partner(a_, HALVES)
+
+    plan = (
+        {
+            "chain": ((take, 1),), "plane": ((share, 1),), "v": ((take, 2), (share, 2)), 1: ((plane, 1),),
+            3: ((diagonal, 1),), 4: ((take, 3), (share, 3)), 5: ((plane, 2),),
+            "feed": ((diagonal, 2), (partners, 1), (partners, 2)), "out": ((plane, 3),),
+            "all": ((diagonal, 3), (partners, 3)),
+        },
+        {
+            "chain": ((take, 2),), "plane": ((lambda a_: rest(), 1), (share, 2)), "q": ((take, 3),),
+            "v": ((plane, 1),), 0: ((share, 3),), 1: ((diagonal, 1),), 2: ((plane, 2),), 4: ((diagonal, 2),),
+            5: ((plane, 3),), "feed": ((partners, 1), (partners, 2)), "out": ((diagonal, 3),), "all": ((partners, 3),),
+        },
+        {
+            "middle": ((take, 3),), "chain": ((plane, 2),), "plane": ((share, 3),), "q": ((take, 1), (share, 1)),
+            "v": ((diagonal, 2),), 2: ((plane, 3),), 4: ((diagonal, 3),), 5: ((plane, 1),),
+            "feed": ((diagonal, 1), (partners, 2), (partners, 1)), "all": ((partners, 3),),
+        },
+        {
+            "middle": ((plane, 3),), "norm": ((take, 2), (share, 2)), "q": ((diagonal, 3),),
+            0: ((take, 1), (share, 1)), 2: ((plane, 2),), 4: ((diagonal, 2),), 5: ((plane, 1),),
+            "feed": ((diagonal, 1), (partners, 3), (partners, 2), (partners, 1)),
+        },
+    )
     pass_chain(0)
-    v_y.wait()
-    vin[2] = vin[1] + vtmp[0]
-    v_x.start()
-    rest(x_copy)
-    pass_chain(1)
-    v_x.wait()
-    vin[3] = vin[2] + vtmp[1]
-    v_core.start()
-    pass_chain(2)
-    v_core.wait()
-    vec[...] = vin[3] + vtmp[2]
+    vec_total = vin[...].astype(f32)
+    for r in range(1, 8):
+        vec_copy(r).wait()
+        vec_total = vec_total + vtmp[r].astype(f32)
+    vec[...] = vec_total
 
     @pl.when(a < nq)
     def _():
@@ -305,8 +344,10 @@
         for h in range(HALVES):
             core(a, b, y, h, HALVES).start()
 
-    for h in range(3, FINE):
+    for h in range(1, FINE):
         pass_chain(h)
+        if h == FINE // 2 - 1:
+            at_slot("middle")
 
     @pl.when(a >= nq)
     def _():
@@ -321,24 +362,15 @@
                 def _():
                     direct(a + d).start()
 
-    if relay:
-        take_at(1)
-
-    @pl.when(a >= nq + 1)
-    def _():
-        pass_plane(a, HALVES)
+    at_slot("chain")
+    if not relay:
+        @pl.when(a >= nq + 1)
+        def _():
+            pass_plane(a, HALVES)
 
     for a_ in range(nq):
         pass_plane(a_, FINE)
-
-    if relay:
-        first = 1 + (a == 1).astype(jnp.int32)
-        second = 2 + ((a == 1) | (a == 2)).astype(jnp.int32)
-
-        @pl.when(a == 0)
-        def _():
-            share(first)
-
+    at_slot("plane")
     loads[2].wait()
 
     @pl.loop(0, SEQ // 256)
@@ -349,26 +381,18 @@
         inverse = lax.rsqrt(jnp.mean(centred * centred, -1, keepdims=True) + EPS)
         n1[at, :] = (centred * inverse * vec[0:1, :] + vec[1:2, :]).astype(bf16)
 
-    @pl.when(a == nq)
-    def _():
-        pass_plane(a, HALVES)
-
-    if relay:
-        take_at(-1)
+    if not relay:
+        @pl.when(a == nq)
+        def _():
+            pass_plane(a, HALVES)
+
+    at_slot("norm")
     for a_ in range(nq):
         pass_diag(a_, FINE)
-    if relay:
-        take_at(2)
     for a_ in range(nq):
         partner(a_, FINE)
     fetch_q = pltpu.make_async_copy(whole.at[pl.ds(0, 3 * D)], wq, wq_sem)
     fetch_q.start()
-    if relay:
-        take_at(-2)
-
-        @pl.when(a > 0)
-        def _():
-            share(first)
 
     def save(k, src, dst):
         return pltpu.make_async_copy(src, dst, save_sem.at[k])
@@ -390,8 +414,10 @@
             qkv[:, at] = r
 
     project(0, 2, 0.125)
+    at_slot("q")
     project(3, None, None)
     project(6, 3, None)
+    at_slot("v")
     save(1, qkv, qkv_out).start()
 
     lo = lax.broadcasted_iota(jnp.int32, (1, 128), 1) < 64
@@ -423,51 +449,22 @@
         lse[i, 0:1, :] = t[0:1]
         lse[i, 1:2, :] = t[64:65]
 
-    def own_diag():
-        @pl.when(a >= nq)
-        def _():
-            pass_diag(a, HALVES)
-
-    def third(act):
-        @pl.when(a == 0)
-        def _():
-            act(3)
-
-    def third_column(a_):
-        take(a_)
-        share(a_)
-
-    steps = ()
-    if relay:
-        steps = (
-            (0, own_diag),
-            (1, lambda: pass_plane(first, HALVES)), (1, lambda: share(second)),
-            (3, lambda: pass_diag(first, HALVES)), (3, lambda: third(third_column)),
-            (4, lambda: pass_plane(second, HALVES)),
-            (5, lambda: pass_diag(second, HALVES)),
-        )
-
     @pl.loop(0, PAIRS)
     def _(i):
         attend(i)
-        for k, act_now in steps:
-            @pl.when(i == k)
-            def _():
-                act_now()
+        for k in range(PAIRS):
+            if relay:
+                @pl.when(i == k)
+                def _():
+                    at_slot(k)
 
     save(2, mixed, mixed_out).start()
-    if relay:
-        partner(first, HALVES)
-
-        @pl.when(a == 0)
-        def _():
-            partner(second, HALVES)
-
-        @pl.when(a > 0)
-        def _():
-            partner(a, HALVES)
-    else:
-        own_diag()
+    at_slot("feed")
+    if not relay:
+        @pl.when(a >= nq)
+        def _():
+            pass_diag(a, HALVES)
+
         for k in range(1, na):
             for a_ in (a + k, a - k):
                 @pl.when((a_ >= nq) & (a_ < na))
@@ -481,22 +478,12 @@
         def _(a_):
             partner(a_, HALVES)
 
-    def settle():
-        if relay:
-            third(lambda a_: pass_diag(a_, HALVES))
-            third(lambda a_: partner(a_, HALVES))
-
-            @pl.when(a > 0)
-            def _():
-                partner(second, HALVES)
-
     fetch_o = pltpu.make_async_copy(whole.at[pl.ds(3 * D, D)], w_out, wq_sem)
     fetch_o.start()
     BLOCKS = FF // 256
-    shift = (a == na - 1).astype(jnp.int32) * 3 if relay else 0
 
     def weights_in(j):
-        at = (j + shift) % BLOCKS * 256
+        at = j * 256
         slot = j % 2
         return (
             pltpu.make_async_copy(whole.at[pl.ds(pl.multiple_of(4 * D + at, 256), 256)], wf.at[slot], w_sem.at[slot]),
@@ -526,8 +513,7 @@
         top_low[at, :] = jnp.where(alive(t), cot[at, :], 0.0).astype(bf16)
         ngrad[at, :] = jnp.zeros((256, D), f32)
 
-    if relay:
-        third(lambda a_: pass_plane(a_, HALVES))
+    at_slot("out")
 
     def put_grad(k, slot, row):
         return pltpu.make_async_copy(
@@ -535,14 +521,14 @@
         )
 
     def put_both(j):
-        at = (j + shift) % BLOCKS * 256
+        at = j * 256
         return put_grad(0, j % 2, D + at), put_grad(1, j % 2, D + FF + at)
 
     @pl.loop(0, BLOCKS)
     def _(j):
         @pl.when(j == 2)
         def _():
-            settle()
+            at_slot("all")
 
         @pl.when(j + 1 < BLOCKS)
         def _():
@@ -552,7 +538,7 @@
         for one in weights_in(j):
             one.wait()
         slot = j % 2
-        unit = (j + shift) % BLOCKS
+        unit = j
         line, cols = 8 + unit // 3, pl.ds(pl.multiple_of(unit % 3 * 256, 256), 256)
         bias = vec[pl.ds(line, 1), cols]
         sums = jnp.zeros((1, 256), f32)
@@ -699,7 +685,7 @@
             pltpu.VMEM((rows, D), bf16), dma,
             pltpu.VMEM((3 * D, D), bf16), dma,
             pltpu.VMEM((16, 128), f32), pltpu.VMEM((na, 16, 128), f32),
-            pltpu.VMEM((4, 16, D), f32), pltpu.VMEM((3, 16, D), f32), dma((3 + na,)), dma((3 + na,)),
+            pltpu.VMEM((16, D), bf16), pltpu.VMEM((8, 16, D), bf16), dma((7 + na,)), dma((7 + na,)),
             pltpu.VMEM((SEQ, 128), f32),
             dma((2 * na, FINE)), dma((na, FINE)), dma((na,)), dma((na,)), dma((na,)),
             dma((na, FINE)), dma((na, FINE)),
@@ -867,7 +853,7 @@
     ]
     for load in loads[:4]:
         load.start()
-    greet(me)
+    greet(me, (me.x_mate(), me.y_mate(), me.core_mate()))
 
     @pl.loop(nq, na)
     def _(a_):
@@ -957,20 +943,31 @@
             stage.at[j % 2], gl.at[pl.ds(pl.multiple_of(j * 256, 256), 256)], stage_sem.at[j % 2]
         )
 
+    def start_saved(low_end, high_end):
+        for a_ in range(nq):
+            for q in range(2):
+                first, size = span(q)
+                for o in range(4):
+                    for core, copy in ((1 - c, to_core), (c, fetch)):
+                        end = me.sid(a_, *around[o], core) * rows + first + size
+
+                        @pl.when((end > low_end) & (end <= high_end))
+                        def _():
+                            copy(a_, o, q).start()
+
     @pl.loop(0, 9)
     def _(j):
         @pl.when(j >= 2)
         def _():
             save(j - 2).wait()
+            start_saved((j - 2) * 256, (j - 1) * 256)
 
         stage[j % 2] = dot(proj[:, pl.ds(pl.multiple_of(j * 256, 256), 256)], n1[...], TN).astype(bf16)
         save(j).start()
 
     save(7).wait()
     save(8).wait()
-    for a_ in range(nq):
-        for q in range(2):
-            start(a_, q)
+    start_saved(7 * 256, 9 * 256)
     for load in loads[5:]:
         load.wait()
 
@@ -988,26 +985,6 @@
         vin[0, 0:1, :] += jnp.sum(g * unit, 0, keepdims=True)
         vin[0, 1:2, :] += jnp.sum(g, 0, keepdims=True)
 
-    def after(t):
-        if t == 0:
-            for a_ in range(nq):
-                for q in range(2):
-                    pair_sum(a_, q)
-        if t == 1:
-            diag_sum(*item(4))
-            spread(*item(3))
-        if t == 2:
-            for a_ in range(nq):
-                diag_sum(a_, 0)
-                diag_sum(a_, 1)
-            pair_sum(*item(5))
-        if t == 3:
-            spread(*item(4))
-
-    for t in range(4):
-        norm_back(t)
-        after(t)
-
     def vec_copy(i, k, peer):
         return pltpu.make_async_remote_copy(
             src_ref=vin.at[i], dst_ref=vtmp.at[k], send_sem=vs.at[k], recv_sem=vr.at[k], device_id=peer
@@ -1018,14 +995,28 @@
     def vec_at(i):
         return vec_copy(3, 2 + i, me.at((a + i) % na))
 
+    late = [(a_, q) for a_ in range(nq) for q in range(2)]
+    norm_back(0)
+    diag_sum(*item(4))
+    for one in late:
+        pair_sum(*one)
+    norm_back(1)
+    spread(*item(3))
+    norm_back(2)
+    diag_sum(*late[0])
+    norm_back(3)
     v_core.start()
-    diag_sum(*item(5))
+    for one in late[1:]:
+        diag_sum(*one)
+    pair_sum(*item(5))
+    spread(*item(4))
     v_core.wait()
     vin[1] = vin[0] + vtmp[0]
     v_y.start()
     for a_ in range(nq):
         link(a_, 0)
         link(a_, 1)
+    diag_sum(*item(5))
     v_y.wait()
     vin[2] = vin[1] + vtmp[1]
     v_x.start()

time: 252 us -> 250 us (level)
  Pallas kernels: 239 us -> 236 us
    pallas_call x1, Pallas kernels: 141 us -> 135 us  [forward(): pl.pallas_call(functools.partial(forward_kernel, n_dp), in_specs=[pl.Bloc...]
where the time goes in v1:
time: 250 us; the launch traced here: 248 us
  Pallas kernels  236 us (94%)
  local copies, waits for them, and re-layouts  5.6 us (2%)
  other arithmetic  5.48 us (2%)
    pallas_call x1, Pallas kernels, forward(): pl.pallas_call(functools.partial(forward_kernel, n_dp), in_specs=[pl.Bloc...  135 us
    pallas_call x1, Pallas kernels, backward(): pl.pallas_call(functools.partial(backward_kernel, n_dp), in_specs=[anyw,...  100 us
    unnamed x12, local copies, waits for them, and re-layouts  5.6 us
    sub x2, other arithmetic, adamw(): return (master - rate * (stride + decay * master), moment_new, square_new)  5.48 us

profile of v1, /device:TPU:0, one launch (start us, length us, event | category | flops | bytes accessed | tf_op | source)
XLA Modules:
  0.0 248.0 jit_solution(13885369973877218437)
XLA Ops:
  1.3 135.4 %gather_forward.1 = (bf16[9216,768]{1,0:T(8,128)(2,1)}, bf16[6912,768]{1,0:T(8,128)(2,1)}, bf16[1024,768]{1,0:T(8,128)(2,1)}, bf16[1024,2304]{1,0:T(8,128)(2,1)}...) custom-call(s32[1]{0:T(128)S(6)} %copy.21.lengths, ...), custom_call_target="tpu_custom_call" | custom-call | tf_op jit(solution)/shard_map/gather_forward/pallas_call | solution.py:671
  136.7 0.0 copy-start
  136.8 100.1 %attend_reduce.1 = (bf16[2304,768]{1,0:T(8,128)(2,1)}, f32[1024,768]{1,0:T(8,128)}, f32[288,768]{1,0:T(8,128)}, f32[16,768]{1,0:T(8,128)}) custom-call(bf16[9216,768]{1,0:T(8,128)(2,1)} %get-tuple-element.25.weights, bf16[6912,768]{1,0:T(8,128)(2,1)} %get-tuple-element.26.ge, bf16[1024,2304]{1,0:T(8,128)(2,1)} %get-tuple-element.27.qkv_in, ...), custom_call_target="tpu_custom_call" | custom-call | tf_op jit(solution)/shard_map/attend_reduce/pallas_call | solution.py:1108
  236.9 0.0 copy-done
  236.9 0.0 copy-start.2
  236.9 0.0 copy-start.3
  236.9 0.0 copy-start.4
  236.9 4.1 %multiply_subtract_fusion = (f32[288,768]{1,0:T(8,128)}, f32[288,768]{1,0:T(8,128)}, f32[288,768]{1,0:T(8,128)}, f32[288,768]{1,0:T(8,128)}) fusion(f32[288,768]{1,0:T(8,128)S(1)} %copy-done, f32[288,768]{1,0:T(8,128)} %get-tuple-element.36, f32[288,768]{1,0:T(8,128)} %param.14, f32[288,768]{1,0:T(8,128)} %param.16), kind=kLoop, calls=%fused_computation | loop fusion | flops 3538944 | bytes 7077888 | tf_op jit(solution)/shard_map/sub | solution.py:1156
  241.0 0.0 copy-done.2
  241.0 0.0 copy-done.3
  241.0 0.0 copy-done.4
  241.0 1.4 multiply_subtract_fusion.1
  242.4 0.0 copy-start.1
  242.4 3.9 %copy.22 = f32[1024,768]{1,0:T(8,128)} copy(f32[1024,768]{1,0:T(8,128)} %get-tuple-element.56) | data formatting | bytes 6291456
  246.3 0.0 copy-done.1
  246.3 1.7 copy.23
Async XLA Ops:
  136.7 100.1 %copy-start = (f32[288,768]{1,0:T(8,128)S(1)}, f32[288,768]{1,0:T(8,128)}, u32[]{:S(2)}) copy-start(f32[288,768]{1,0:T(8,128)} %master_in.1) | copy-start | bytes 2654212
  236.9 4.1 %copy-start.2 = (f32[12,24]{1,0:T(8,128)S(1)}, f32[12,24]{1,0:T(8,128)}, u32[]{:S(2)}) copy-start(f32[12,24]{1,0:T(8,128)} %vector_in.1) | copy-start | bytes 3460
  236.9 4.1 %copy-start.3 = (f32[12,24]{1,0:T(8,128)S(1)}, f32[12,24]{1,0:T(8,128)}, u32[]{:S(2)}) copy-start(f32[12,24]{1,0:T(8,128)} %param.15) | copy-start | bytes 3460
  236.9 4.1 %copy-start.4 = (f32[12,24]{1,0:T(8,128)S(1)}, f32[12,24]{1,0:T(8,128)}, u32[]{:S(2)}) copy-start(f32[12,24]{1,0:T(8,128)} %param.17) | copy-start | bytes 3460
  242.4 3.9 %copy-start.1 = (f32[1024,768]{1,0:T(8,128)S(1)}, f32[1024,768]{1,0:T(8,128)}, u32[]{:S(2)}) copy-start(f32[1024,768]{1,0:T(8,128)} %get-tuple-element.57) | copy-start | bytes 9437188

commit v2 on v1

--- a/solution.py
+++ b/solution.py
@@ -307,7 +307,7 @@
     plan = (
         {
             "chain": ((take, 1),), "plane": ((share, 1),), "v": ((take, 2), (share, 2)), 1: ((plane, 1),),
-            3: ((diagonal, 1),), 4: ((take, 3), (share, 3)), 5: ((plane, 2),),
+            3: ((diagonal, 1),), 4: ((plane, 2), (take, 3), (share, 3)),
             "feed": ((diagonal, 2), (partners, 1), (partners, 2)), "out": ((plane, 3),),
             "all": ((diagonal, 3), (partners, 3)),
         },
@@ -317,23 +317,17 @@
             5: ((plane, 3),), "feed": ((partners, 1), (partners, 2)), "out": ((diagonal, 3),), "all": ((partners, 3),),
         },
         {
-            "middle": ((take, 3),), "chain": ((plane, 2),), "plane": ((share, 3),), "q": ((take, 1), (share, 1)),
-            "v": ((diagonal, 2),), 2: ((plane, 3),), 4: ((diagonal, 3),), 5: ((plane, 1),),
+            "middle": ((take, 3),), "chain": ((plane, 2),), "plane": ((share, 3),), "norm": ((take, 1),), "q": ((share, 1),),
+            "v": ((diagonal, 2),), 2: ((plane, 3),), 3: ((plane, 1),), 4: ((diagonal, 3),),
             "feed": ((diagonal, 1), (partners, 2), (partners, 1)), "all": ((partners, 3),),
         },
         {
-            "middle": ((plane, 3),), "norm": ((take, 2), (share, 2)), "q": ((diagonal, 3),),
-            0: ((take, 1), (share, 1)), 2: ((plane, 2),), 4: ((diagonal, 2),), 5: ((plane, 1),),
+            "middle": ((plane, 3),), "norm": ((take, 2), (share, 2)), "q": ((diagonal, 3), (take, 1), (share, 1)),
+            1: ((plane, 2),), 3: ((plane, 1),), 4: ((diagonal, 2),),
             "feed": ((diagonal, 1), (partners, 3), (partners, 2), (partners, 1)),
         },
     )
     pass_chain(0)
-    vec_total = vin[...].astype(f32)
-    for r in range(1, 8):
-        vec_copy(r).wait()
-        vec_total = vec_total + vtmp[r].astype(f32)
-    vec[...] = vec_total
-
     @pl.when(a < nq)
     def _():
         for h in range(FINE):
@@ -371,6 +365,11 @@
     for a_ in range(nq):
         pass_plane(a_, FINE)
     at_slot("plane")
+    vec_total = vin[...].astype(f32)
+    for r in range(1, 8):
+        vec_copy(r).wait()
+        vec_total = vec_total + vtmp[r].astype(f32)
+    vec[...] = vec_total
     loads[2].wait()
 
     @pl.loop(0, SEQ // 256)
@@ -841,7 +840,7 @@
             chain(a_, h, False).start()
 
     def item(i):
-        return nq + i // 2 + 0 * a, i % 2
+        return nq + (i // 2 + 2) % 3 + 0 * a, i % 2
 
     def local(k, src, dst):
         return pltpu.make_async_copy(src, dst, load_sem.at[k])
@@ -937,6 +936,7 @@
                 act(*item(which))
 
     loads[4].wait()
+    pair_sum(*item(5))
 
     def save(j):
         return pltpu.make_async_copy(
@@ -1008,15 +1008,14 @@
     v_core.start()
     for one in late[1:]:
         diag_sum(*one)
-    pair_sum(*item(5))
     spread(*item(4))
     v_core.wait()
     vin[1] = vin[0] + vtmp[0]
     v_y.start()
+    diag_sum(*item(5))
     for a_ in range(nq):
         link(a_, 0)
         link(a_, 1)
-    diag_sum(*item(5))
     v_y.wait()
     vin[2] = vin[1] + vtmp[1]
     v_x.start()

time: 250 us -> 243 us (0.972)
  Pallas kernels: 236 us -> 230 us
    pallas_call x1, Pallas kernels: 135 us -> 129 us  [forward(): pl.pallas_call(functools.partial(forward_kernel, n_dp), in_specs=[pl.Bloc...]
where the time goes in v2:
time: 243 us
  Pallas kernels  230 us (95%)
  local copies, waits for them, and re-layouts  5.6 us (2%)
  other arithmetic  5.48 us (2%)
    pallas_call x1, Pallas kernels, forward(): pl.pallas_call(functools.partial(forward_kernel, n_dp), in_specs=[pl.Bloc...  129 us
    pallas_call x1, Pallas kernels, backward(): pl.pallas_call(functools.partial(backward_kernel, n_dp), in_specs=[anyw,...  102 us
    unnamed x12, local copies, waits for them, and re-layouts  5.6 us
    sub x2, other arithmetic, adamw(): return (master - rate * (stride + decay * master), moment_new, square_new)  5.48 us

profile of v2, /device:TPU:0, one launch (start us, length us, event | category | flops | bytes accessed | tf_op | source)
XLA Modules:
  0.0 242.9 jit_solution(7110373484256728277)
XLA Ops:
  1.3 128.5 %gather_forward.1 = (bf16[9216,768]{1,0:T(8,128)(2,1)}, bf16[6912,768]{1,0:T(8,128)(2,1)}, bf16[1024,768]{1,0:T(8,128)(2,1)}, bf16[1024,2304]{1,0:T(8,128)(2,1)}...) custom-call(s32[1]{0:T(128)S(6)} %copy.21.lengths, ...), custom_call_target="tpu_custom_call" | custom-call | tf_op jit(solution)/shard_map/gather_forward/pallas_call | solution.py:670
  129.8 0.0 copy-start
  129.8 101.9 %attend_reduce.1 = (bf16[2304,768]{1,0:T(8,128)(2,1)}, f32[1024,768]{1,0:T(8,128)}, f32[288,768]{1,0:T(8,128)}, f32[16,768]{1,0:T(8,128)}) custom-call(bf16[9216,768]{1,0:T(8,128)(2,1)} %get-tuple-element.25.weights, bf16[6912,768]{1,0:T(8,128)(2,1)} %get-tuple-element.26.ge, bf16[1024,2304]{1,0:T(8,128)(2,1)} %get-tuple-element.27.qkv_in, ...), custom_call_target="tpu_custom_call" | custom-call | tf_op jit(solution)/shard_map/attend_reduce/pallas_call | solution.py:1107
  231.8 0.0 copy-done
  231.8 0.0 copy-start.2
  231.8 0.0 copy-start.3
  231.8 0.0 copy-start.4
  231.8 4.1 %multiply_subtract_fusion = (f32[288,768]{1,0:T(8,128)}, f32[288,768]{1,0:T(8,128)}, f32[288,768]{1,0:T(8,128)}, f32[288,768]{1,0:T(8,128)}) fusion(f32[288,768]{1,0:T(8,128)S(1)} %copy-done, f32[288,768]{1,0:T(8,128)} %get-tuple-element.36, f32[288,768]{1,0:T(8,128)} %param.14, f32[288,768]{1,0:T(8,128)} %param.16), kind=kLoop, calls=%fused_computation | loop fusion | flops 3538944 | bytes 7077888 | tf_op jit(solution)/shard_map/sub | solution.py:1155
  235.9 0.0 copy-done.2
  235.9 0.0 copy-done.3
  235.9 0.0 copy-done.4
  235.9 1.4 multiply_subtract_fusion.1
  237.3 0.0 copy-start.1
  237.3 3.9 %copy.22 = f32[1024,768]{1,0:T(8,128)} copy(f32[1024,768]{1,0:T(8,128)} %get-tuple-element.56) | data formatting | bytes 6291456
  241.2 0.0 copy-done.1
  241.2 1.7 copy.23
Async XLA Ops:
  129.8 102.0 %copy-start = (f32[288,768]{1,0:T(8,128)S(1)}, f32[288,768]{1,0:T(8,128)}, u32[]{:S(2)}) copy-start(f32[288,768]{1,0:T(8,128)} %master_in.1) | copy-start | bytes 2654212
  231.8 4.1 %copy-start.2 = (f32[12,24]{1,0:T(8,128)S(1)}, f32[12,24]{1,0:T(8,128)}, u32[]{:S(2)}) copy-start(f32[12,24]{1,0:T(8,128)} %vector_in.1) | copy-start | bytes 3460
  231.8 4.1 %copy-start.3 = (f32[12,24]{1,0:T(8,128)S(1)}, f32[12,24]{1,0:T(8,128)}, u32[]{:S(2)}) copy-start(f32[12,24]{1,0:T(8,128)} %param.15) | copy-start | bytes 3460
  231.8 4.1 %copy-start.4 = (f32[12,24]{1,0:T(8,128)S(1)}, f32[12,24]{1,0:T(8,128)}, u32[]{:S(2)}) copy-start(f32[12,24]{1,0:T(8,128)} %param.17) | copy-start | bytes 3460
  237.3 3.9 %copy-start.1 = (f32[1024,768]{1,0:T(8,128)S(1)}, f32[1024,768]{1,0:T(8,128)}, u32[]{:S(2)}) copy-start(f32[1024,768]{1,0:T(8,128)} %get-tuple-element.57) | copy-start | bytes 9437188
